TPU v7x, 32 devices: a whole 2x2x4 slice. The times are simulated.
32 devices in a mesh: ep: 4 (over y, x), edp: 4 (over z), tp: 2 (over core).
Axes of the slice: x: 2, y: 2, z: 4, core: 2. Of those that a mesh axis runs over, the one named last changes fastest.
Arguments:
- tokens: bfloat16 [2048, 4096], P(('ep', 'edp'), 'tp'), may hold values from -6 to 6
- cotangent: bfloat16 [2048, 4096], P(('ep', 'edp'), 'tp'), may hold values from -6 to 6
- expert_ids: int32 [2048, 8], P(('ep', 'edp')), may hold values from 0 to 127, all different within a row; in each aligned block of 128 rows (0 to 127, 128 to 255, ...) at most 10 rows name the same one
- route_weights: float32 [2048, 8], P(('ep', 'edp')), may hold values from 0.1 to 1
- expert_weights: bfloat16 [3, 1536, 4096], P(None, ('ep', 'tp')), may hold values from -0.15625 to 0.15625
Outputs:
- mixed: bfloat16 [2048, 4096], P(('ep', 'edp'), 'tp')
- grad_tokens: bfloat16 [2048, 4096], P(('ep', 'edp'), 'tp')
- weight_grads: float32 [3, 1536, 4096], P(None, ('ep', 'tp'), 'edp')
Inputs may be any that keep to these rules, and one draw needn't show every extreme that they name: `expert_ids`: each token names 8 different experts; within the tokens of one (ep, edp) index no expert is named by more than 10 tokens.
All inputs are finite; a program needn't handle non-finite values.
Results may differ from a plain program's by a relative error of at most 0.017.
Values may be sent and summed in bfloat16 or wider, within the bound.
A program may use at most 64 MiB of HBM per device.

v0:
```python
import jax
import jax.numpy as jnp
from jax import lax
from jax.sharding import PartitionSpec as P

CAP = 10


def route_tables(expert_ids, route_weights, window):
    tok_rows, top_count = expert_ids.shape
    flat_ids = expert_ids.reshape(-1)
    matches = (flat_ids[:, None] == jnp.arange(window, dtype=jnp.int32)[None, :]).astype(jnp.int32)
    slot_index = jnp.sum(matches * (jnp.cumsum(matches, axis=0) - 1), axis=1)
    in_slot = (slot_index[:, None] == jnp.arange(CAP, dtype=jnp.int32)[None, :]).astype(jnp.float32)
    placed = matches.astype(jnp.float32)[:, :, None] * in_slot[:, None, :]
    placed = placed.reshape(tok_rows, top_count, window, CAP)
    select = jnp.sum(placed, axis=1)
    weighted = jnp.sum(placed * route_weights[:, :, None, None], axis=1)
    return (select, weighted)


def pack_rows(select, weighted, features, grads_in):
    packed = jnp.einsum(
        "tec,td->ecd", select.astype(jnp.bfloat16), features, preferred_element_type=jnp.float32
    ).astype(jnp.bfloat16)
    scaled = jnp.einsum(
        "tec,td->ecd", weighted, grads_in.astype(jnp.float32), precision=lax.Precision.HIGHEST
    ).astype(jnp.bfloat16)
    return (jnp.repeat(packed, 4, axis=0), jnp.repeat(scaled, 4, axis=0))


def replica_sum(left, right):
    partial_sums = jnp.einsum("prs,prd->psd", left, right, preferred_element_type=jnp.float32)
    rounded = lax.optimization_barrier(partial_sums.astype(jnp.bfloat16)).astype(jnp.float32)
    return jnp.sum(rounded, axis=0)


def shards(tokens, cotangent, expert_ids, route_weights, expert_weights):
    n_devices = lax.axis_size("ep")
    window = n_devices // 4
    select, weighted = route_tables(expert_ids, route_weights, window)
    whole_tokens, whole_grads = (
        lax.all_gather(tokens, "tp", axis=1, tiled=True),
        lax.all_gather(cotangent, "tp", axis=1, tiled=True),
    )
    packed, scaled = pack_rows(select, weighted, whole_tokens, whole_grads)
    rows_in, grads_in = (
        lax.all_to_all(packed, "ep", split_axis=0, concat_axis=0, tiled=True),
        lax.all_to_all(scaled, "ep", split_axis=0, concat_axis=0, tiled=True),
    )
    width = rows_in.shape[2]
    token_rows = rows_in.reshape(-1, width)
    grad_rows = grads_in.reshape(-1, width)
    gate_up = jnp.einsum(
        "rd,jfd->jrf", token_rows, expert_weights[:2], preferred_element_type=jnp.float32
    )
    gate_val = gate_up[0]
    up_val = gate_up[1]
    gate_weight = expert_weights[0]
    up_weight = expert_weights[1]
    down_weight = expert_weights[2]
    sigmoid_gate = jax.nn.sigmoid(gate_val)
    active = gate_val * sigmoid_gate
    hidden = (active * up_val).astype(jnp.bfloat16)
    out_part = jnp.dot(hidden, down_weight, preferred_element_type=jnp.float32)
    contract_last = (((1,), (1,)), ((), ()))
    d_hidden = lax.dot_general(
        grad_rows, down_weight, contract_last, preferred_element_type=jnp.float32
    )
    d_gate = (d_hidden * up_val * sigmoid_gate * (1.0 + gate_val * (1.0 - sigmoid_gate))).astype(
        jnp.bfloat16
    )
    d_up = (d_hidden * active).astype(jnp.bfloat16)
    back_part = jnp.dot(d_gate, gate_weight, preferred_element_type=jnp.float32) + jnp.dot(
        d_up, up_weight, preferred_element_type=jnp.float32
    )
    replicas = lax.axis_size("edp")
    rows_block, grads_block = (
        lax.all_to_all(token_rows, "edp", split_axis=1, concat_axis=0, tiled=True),
        lax.all_to_all(grad_rows, "edp", split_axis=1, concat_axis=0, tiled=True),
    )
    left_factors = lax.all_gather(jnp.stack([d_gate, d_up, hidden]), "edp", axis=1, tiled=True)
    block_width = rows_block.shape[1]
    rows_block = rows_block.reshape(replicas, -1, block_width)
    grads_block = grads_block.reshape(replicas, -1, block_width)
    left_factors = left_factors.reshape(3, replicas, -1, left_factors.shape[2])
    weight_grads = jnp.stack(
        [
            replica_sum(left_factors[0], rows_block),
            replica_sum(left_factors[1], rows_block),
            replica_sum(left_factors[2], grads_block),
        ]
    )
    out_sum, back_sum = (
        lax.psum_scatter(
            out_part.astype(jnp.bfloat16), "tp", scatter_dimension=1, tiled=True
        ).astype(jnp.float32),
        lax.psum_scatter(
            back_part.astype(jnp.bfloat16), "tp", scatter_dimension=1, tiled=True
        ).astype(jnp.float32),
    )
    home_out, home_back = (
        lax.all_to_all(
            out_sum.astype(jnp.bfloat16).reshape(n_devices, CAP, -1),
            "ep",
            split_axis=0,
            concat_axis=0,
            tiled=True,
        ),
        lax.all_to_all(
            back_sum.astype(jnp.bfloat16).reshape(n_devices, CAP, -1),
            "ep",
            split_axis=0,
            concat_axis=0,
            tiled=True,
        ),
    )
    pair_out = home_out.astype(jnp.float32).reshape(window, 4, CAP, -1).sum(axis=1)
    pair_back = home_back.astype(jnp.float32).reshape(window, 4, CAP, -1).sum(axis=1)
    mixed = jnp.einsum("tec,ecd->td", weighted, pair_out, precision=lax.Precision.HIGHEST).astype(
        jnp.bfloat16
    )
    grad_tokens = jnp.einsum(
        "tec,ecd->td", select, pair_back, precision=lax.Precision.HIGHEST
    ).astype(jnp.bfloat16)
    return (mixed, grad_tokens, weight_grads)


def solution(mesh):
    placed = (
        P(("ep", "edp"), "tp"),
        P(("ep", "edp"), "tp"),
        P(("ep", "edp"), None),
        P(("ep", "edp"), None),
        P(None, ("ep", "tp"), None),
    )
    return jax.shard_map(
        shards,
        mesh=mesh,
        in_specs=placed,
        out_specs=(P(("ep", "edp"), "tp"), P(("ep", "edp"), "tp"), P(None, ("ep", "tp"), "edp")),
        check_vma=False,
    )
```

profile of v0, /device:TPU:0, one launch (start us, length us, event | category | flops | bytes accessed | tf_op | source)
XLA Modules:
  0.0 122.3 jit_solution(8222102204199329675)
XLA Ops:
  11.3 10.0 %all-gather.3.cloned.1.call-done = bf16[128,4096]{1,0:T(8,128)(2,1)} async-done(((bf16[128,2048]{1,0:T(8,128)(2,1)}), bf16[128,4096]{1,0:T(8,128)(2,1)}) %all-gather.3.cloned.1.call-update) | async-done | bytes 1048592 | tf_op jit(solution)/shard_map/all_gather | solution.py:43
  23.6 3.9 %all-to-all-start = ((bf16[4,10,4096]{2,1,0:T(8,128)(2,1)}), bf16[4,10,4096]{2,1,0:T(8,128)(2,1)S(1)}, u32[]{:S(2)}, u32[]{:S(2)}) async-start(bf16[4,10,4096]{2,1,0:T(8,128)(2,1)} %reshape.215), calls=%async_computation | async-start | bytes 1048576 | tf_op jit(solution)/shard_map/all_to_all | solution.py:48
  27.6 5.5 %all-gather.5.cloned.1.call-done = bf16[128,4096]{1,0:T(8,128)(2,1)} async-done(((bf16[128,2048]{1,0:T(8,128)(2,1)}), bf16[128,4096]{1,0:T(8,128)(2,1)}) %all-gather.5.cloned.1.call-update) | async-done | bytes 1048592 | tf_op jit(solution)/shard_map/all_gather | solution.py:44
  33.1 1.7 %convolution_convert_fusion.1 = bf16[10,4096]{1,0:T(8,128)(2,1)S(1)} fusion(f32[128,10]{0,1:T(8,128)S(1)} %get-tuple-element.4, bf16[128,4096]{1,0:T(8,128)(2,1)} %all-gather.5.cloned.1.call-done), kind=kOutput, calls=%fused_computation.3 | convolution fusion | flops 62955520 | bytes 1135616 | tf_op jit(solution)/shard_map/tec,td->ecd/dot_general | solution.py:26
  36.9 3.5 %all-to-all-start.2 = ((bf16[4,10,4096]{2,1,0:T(8,128)(2,1)}), bf16[4,10,4096]{2,1,0:T(8,128)(2,1)S(1)}, u32[]{:S(2)}, u32[]{:S(2)}) async-start(bf16[4,10,4096]{2,1,0:T(8,128)(2,1)} %reshape.218), calls=%async_computation.3 | async-start | bytes 1048576 | tf_op jit(solution)/shard_map/all_to_all | solution.py:49
  40.5 3.0 %fusion.13 = f32[2,40,192]{2,1,0:T(8,128)S(1)} fusion(bf16[40,4096,1]{1,0,2:T(8,128)(2,1)S(1)} %reshape.222, bf16[3,192,4096]{2,1,0:T(8,128)(2,1)} %param.9), kind=kOutput, calls=%fused_computation.26 | convolution fusion | flops 125829120 | bytes 3534848 | tf_op jit(solution)/shard_map/rd,jfd->jrf/dot_general | solution.py:54
  43.5 4.6 %all-to-all-done.2 = bf16[4,10,4096]{2,1,0:T(8,128)(2,1)S(1)} async-done(((bf16[4,10,4096]{2,1,0:T(8,128)(2,1)}), bf16[4,10,4096]{2,1,0:T(8,128)(2,1)S(1)}, u32[]{:S(2)}, u32[]{:S(2)}) %all-to-all-start.2) | async-done | bytes 327712 | tf_op jit(solution)/shard_map/all_to_all | solution.py:49
  48.2 2.0 %fusion.27 = (bf16[40,192]{1,0:T(8,128)(2,1)S(1)}, bf16[40,192]{1,0:T(8,128)(2,1)S(1)}) fusion(f32[2,40,192]{2,1,0:T(8,128)S(1)} %fusion.13, bf16[40,4096]{1,0:T(8,128)(2,1)S(1)} %reshape.219, bf16[3,192,4096]{2,1,0:T(8,128)(2,1)} %param.9), kind=kOutput, calls=%fused_computation.46 | convolution fusion | flops 63014400 | bytes 1992704 | tf_op jit(solution)/shard_map/dot_general | solution.py:67
  50.2 1.8 %fusion.4 = f32[40,4096]{1,0:T(8,128)S(1)} fusion(bf16[40,192]{1,0:T(8,128)(2,1)S(1)} %get-tuple-element.11, bf16[3,192,4096]{2,1,0:T(8,128)(2,1)} %param.9), kind=kOutput, calls=%fused_computation.17 | convolution fusion | flops 62914560 | bytes 2243584 | tf_op jit(solution)/shard_map/dot_general | solution.py:74
  52.0 2.5 %fusion = bf16[40,4096]{1,0:T(8,128)(2,1)} fusion(f32[40,4096]{1,0:T(8,128)S(1)} %fusion.4, bf16[40,192]{1,0:T(8,128)(2,1)S(1)} %get-tuple-element.10, bf16[3,192,4096]{2,1,0:T(8,128)(2,1)} %param.9), kind=kOutput, calls=%fused_computation.1 | convolution fusion | flops 63242240 | bytes 2571264 | tf_op jit(solution)/shard_map/dot_general | solution.py:74
  55.6 4.7 %all-to-all-start.4 = ((bf16[40,4,1024]{2,0,1:T(8,128)(2,1)}), bf16[40,4,1024]{2,0,1:T(8,128)(2,1)S(1)}, u32[]{:S(2)}, u32[]{:S(2)}) async-start(bf16[40,4,1024]{2,0,1:T(8,128)(2,1)} %copy.30), calls=%async_computation.6 | async-start | bytes 655360 | tf_op jit(solution)/shard_map/all_to_all | solution.py:79
  60.3 2.5 %convolution_convert_fusion = bf16[40,4096]{1,0:T(8,128)(2,1)} fusion(bf16[3,192,4096]{2,1,0:T(8,128)(2,1)} %param.9, bf16[1,40,192]{2,1,0:T(8,128)(2,1)S(1)} %multiply_convert_fusion), kind=kOutput, calls=%fused_computation.2 | convolution fusion | flops 63078400 | bytes 1915904 | tf_op jit(solution)/shard_map/dot_general | solution.py:65
  64.0 14.8 %all_gather.11 = bf16[3,160,192]{2,1,0:T(8,128)(2,1)S(1)} all-gather(bf16[3,40,192]{2,1,0:T(8,128)(2,1)S(1)} %pad_maximum_fusion.1), channel_id=1, replica_groups=mesh['ep'=4,'edp'=4,'tp'=2] {'edp'}, dimensions={1}, use_global_device_ids=true | all-gather | bytes 230400 | tf_op jit(solution)/shard_map/all_gather | solution.py:82
  79.5 4.1 %all-to-all-start.5 = ((bf16[40,4,1024]{2,0,1:T(8,128)(2,1)}), bf16[40,4,1024]{2,0,1:T(8,128)(2,1)}, u32[]{:S(2)}, u32[]{:S(2)}) async-start(bf16[40,4,1024]{2,0,1:T(8,128)(2,1)} %copy.31), calls=%async_computation.7 | async-start | bytes 655360 | tf_op jit(solution)/shard_map/all_to_all | solution.py:80
  85.7 5.3 %all-to-all-done.5 = bf16[40,4,1024]{2,0,1:T(8,128)(2,1)} async-done(((bf16[40,4,1024]{2,0,1:T(8,128)(2,1)}), bf16[40,4,1024]{2,0,1:T(8,128)(2,1)}, u32[]{:S(2)}, u32[]{:S(2)}) %all-to-all-start.5) | async-done | bytes 327712 | tf_op jit(solution)/shard_map/all_to_all | solution.py:80
  91.0 1.6 %convolution_convert_fusion.5 = bf16[4,192,1024]{2,1,0:T(8,128)(2,1)S(1)} fusion(bf16[4,40,192]{2,1,0:T(8,128)(2,1)S(1)} %bitcast.86, bf16[40,4,1024]{2,0,1:T(8,128)(2,1)} %all-to-all-done.5), kind=kOutput, calls=%fused_computation.13 | convolution fusion | flops 63700992 | bytes 1961984 | tf_op jit(solution)/shard_map/prs,prd->psd/dot_general | solution.py:33
  94.3 1.7 %reshape.220 = bf16[4,10,2048]{2,1,0:T(8,128)(2,1)} reshape(bf16[40,2048]{1,0:T(8,128)(2,1)} %reduce-scatter.5.cloned.1.call-done) | data formatting | bytes 327680 | tf_op jit(solution)/shard_map/reshape | solution.py:111
  96.0 3.4 %all-to-all-start.3 = ((bf16[4,10,2048]{2,1,0:T(8,128)(2,1)}), bf16[4,10,2048]{2,1,0:T(8,128)(2,1)S(1)}, u32[]{:S(2)}, u32[]{:S(2)}) async-start(bf16[4,10,2048]{2,1,0:T(8,128)(2,1)} %reshape.220), calls=%async_computation.5 | async-start | bytes 524288 | tf_op jit(solution)/shard_map/all_to_all | solution.py:110
  101.0 1.7 %reshape.217 = bf16[4,10,2048]{2,1,0:T(8,128)(2,1)} reshape(bf16[40,2048]{1,0:T(8,128)(2,1)} %reduce-scatter.3.cloned.1.call-done) | data formatting | bytes 327680 | tf_op jit(solution)/shard_map/reshape | solution.py:104
  102.7 2.4 %all-to-all-done.3 = bf16[4,10,2048]{2,1,0:T(8,128)(2,1)S(1)} async-done(((bf16[4,10,2048]{2,1,0:T(8,128)(2,1)}), bf16[4,10,2048]{2,1,0:T(8,128)(2,1)S(1)}, u32[]{:S(2)}, u32[]{:S(2)}) %all-to-all-start.3) | async-done | bytes 163872 | tf_op jit(solution)/shard_map/all_to_all | solution.py:110
  105.1 3.4 %all-to-all-start.1 = ((bf16[4,10,2048]{2,1,0:T(8,128)(2,1)}), bf16[4,10,2048]{2,1,0:T(8,128)(2,1)S(1)}, u32[]{:S(2)}, u32[]{:S(2)}) async-start(bf16[4,10,2048]{2,1,0:T(8,128)(2,1)} %reshape.217), calls=%async_computation.2 | async-start | bytes 524288 | tf_op jit(solution)/shard_map/all_to_all | solution.py:103
  108.6 1.8 %convolution_convert_fusion.3 = bf16[128,2048]{1,0:T(8,128)(2,1)} fusion(f32[128,10]{0,1:T(8,128)S(1)} %copy-done.4, f32[10,2048]{1,0:T(8,128)S(1)} %convert_reduce_fusion.3), kind=kOutput, calls=%fused_computation.10 | convolution fusion | flops 31719424 | bytes 611328 | tf_op jit(solution)/shard_map/tec,ecd->td/dot_general | solution.py:123
  110.4 3.5 %all-to-all-done.1 = bf16[4,10,2048]{2,1,0:T(8,128)(2,1)S(1)} async-done(((bf16[4,10,2048]{2,1,0:T(8,128)(2,1)}), bf16[4,10,2048]{2,1,0:T(8,128)(2,1)S(1)}, u32[]{:S(2)}, u32[]{:S(2)}) %all-to-all-start.1) | async-done | bytes 163872 | tf_op jit(solution)/shard_map/all_to_all | solution.py:103
  113.9 1.8 %convolution_convert_fusion.4 = bf16[128,2048]{1,0:T(8,128)(2,1)} fusion(f32[128,10]{0,1:T(8,128)S(1)} %copy-done.2, f32[10,2048]{1,0:T(8,128)S(1)} %convert_reduce_fusion.4), kind=kOutput, calls=%fused_computation.11 | convolution fusion | flops 31719424 | bytes 611328 | tf_op jit(solution)/shard_map/tec,ecd->td/dot_general | solution.py:120
  (57 shorter events, 17.0 us)
Async XLA Ops:
  7.2 14.2 %all-gather.3.cloned.1.call-start = ((), (), s32[]{:S(2)}) async-start(), calls=%async_computation.8 | async-start | bytes 1572864 | tf_op jit(solution)/shard_map/all_gather | solution.py:43
  7.9 25.2 %all-gather.5.cloned.1.call-start = ((), (), s32[]{:S(2)}) async-start(), calls=%async_computation.10 | async-start | bytes 1572864 | tf_op jit(solution)/shard_map/all_gather | solution.py:44
  11.3 12.3 %copy-start.3 = (f32[128,10]{0,1:T(8,128)}, f32[128,10]{0,1:T(8,128)S(1)}, u32[]{:S(2)}) copy-start(f32[128,10]{0,1:T(8,128)S(1)} %get-tuple-element.3) | copy-start | bytes 15364
  11.3 25.5 %copy-start.1 = (f32[128,10]{0,1:T(8,128)}, f32[128,10]{0,1:T(8,128)S(1)}, u32[]{:S(2)}) copy-start(f32[128,10]{0,1:T(8,128)S(1)} %get-tuple-element.4) | copy-start | bytes 15364
  23.6 12.4 %all-to-all-start = ((bf16[4,10,4096]{2,1,0:T(8,128)(2,1)}), bf16[4,10,4096]{2,1,0:T(8,128)(2,1)S(1)}, u32[]{:S(2)}, u32[]{:S(2)}) async-start(bf16[4,10,4096]{2,1,0:T(8,128)(2,1)} %reshape.215), calls=%async_computation | async-start | bytes 1048576 | tf_op jit(solution)/shard_map/all_to_all | solution.py:48
  36.9 11.2 %all-to-all-start.2 = ((bf16[4,10,4096]{2,1,0:T(8,128)(2,1)}), bf16[4,10,4096]{2,1,0:T(8,128)(2,1)S(1)}, u32[]{:S(2)}, u32[]{:S(2)}) async-start(bf16[4,10,4096]{2,1,0:T(8,128)(2,1)} %reshape.218), calls=%async_computation.3 | async-start | bytes 1048576 | tf_op jit(solution)/shard_map/all_to_all | solution.py:49
  40.3 54.0 %reduce-scatter.5.cloned.1.call-start = ((), (), s32[]{:S(2)}) async-start(), calls=%async_computation.11 | async-start | bytes 491520 | tf_op jit(solution)/shard_map/reduce_scatter | solution.py:98
  55.6 23.8 %all-to-all-start.4 = ((bf16[40,4,1024]{2,0,1:T(8,128)(2,1)}), bf16[40,4,1024]{2,0,1:T(8,128)(2,1)S(1)}, u32[]{:S(2)}, u32[]{:S(2)}) async-start(bf16[40,4,1024]{2,0,1:T(8,128)(2,1)} %copy.30), calls=%async_computation.6 | async-start | bytes 655360 | tf_op jit(solution)/shard_map/all_to_all | solution.py:79
  60.3 40.7 %reduce-scatter.3.cloned.1.call-start = ((), (), s32[]{:S(2)}) async-start(), calls=%async_computation.9 | async-start | bytes 491520 | tf_op jit(solution)/shard_map/reduce_scatter | solution.py:95
  79.5 11.5 %all-to-all-start.5 = ((bf16[40,4,1024]{2,0,1:T(8,128)(2,1)}), bf16[40,4,1024]{2,0,1:T(8,128)(2,1)}, u32[]{:S(2)}, u32[]{:S(2)}) async-start(bf16[40,4,1024]{2,0,1:T(8,128)(2,1)} %copy.31), calls=%async_computation.7 | async-start | bytes 655360 | tf_op jit(solution)/shard_map/all_to_all | solution.py:80
  93.7 5.7 %copy-start = (f32[192,1024]{1,0:T(8,128)S(1)}, f32[192,1024]{1,0:T(8,128)}, u32[]{:S(2)}) copy-start(f32[192,1024]{1,0:T(8,128)} %convert_reduce_fusion.2) | copy-start | bytes 2359300
  96.0 9.1 %all-to-all-start.3 = ((bf16[4,10,2048]{2,1,0:T(8,128)(2,1)}), bf16[4,10,2048]{2,1,0:T(8,128)(2,1)S(1)}, u32[]{:S(2)}, u32[]{:S(2)}) async-start(bf16[4,10,2048]{2,1,0:T(8,128)(2,1)} %reshape.220), calls=%async_computation.5 | async-start | bytes 524288 | tf_op jit(solution)/shard_map/all_to_all | solution.py:110
  99.4 9.1 %copy-start.4 = (f32[128,10]{0,1:T(8,128)S(1)}, f32[128,10]{0,1:T(8,128)}, u32[]{:S(2)}) copy-start(f32[128,10]{0,1:T(8,128)} %copy-done.3) | copy-start | bytes 15364
  101.0 12.9 %copy-start.2 = (f32[128,10]{0,1:T(8,128)S(1)}, f32[128,10]{0,1:T(8,128)}, u32[]{:S(2)}) copy-start(f32[128,10]{0,1:T(8,128)} %copy-done.1) | copy-start | bytes 15364
  105.1 8.8 %all-to-all-start.1 = ((bf16[4,10,2048]{2,1,0:T(8,128)(2,1)}), bf16[4,10,2048]{2,1,0:T(8,128)(2,1)S(1)}, u32[]{:S(2)}, u32[]{:S(2)}) async-start(bf16[4,10,2048]{2,1,0:T(8,128)(2,1)} %reshape.217), calls=%async_computation.2 | async-start | bytes 524288 | tf_op jit(solution)/shard_map/all_to_all | solution.py:103
Sparse Core Ops, SparseCore 0:
  9.5 11.7 all-gather.2
  22.9 10.1 all-gather.4
  54.7 7.8 reduce-scatter.4
  65.3 8.8 reduce-scatter.2
where the time goes:
time: 123 us; the launch traced here: 122 us
  waiting for transfers between devices  33.9 us (28%)
  starting transfers between devices  23.1 us (19%)
  matrix products  22.4 us (18%)
  blocking collectives  14.8 us (12%)
  between operations  14 us (11%)
  local copies, waits for them, and re-layouts  8.74 us (7%)
  other arithmetic  5.3 us (4%)
    all_gather x1, blocking collectives, shards(): lax.all_gather(jnp.stack([d_gate, d_up, hidden]), 'edp', axis=1, tiled=True)  14.8 us
    all_gather x1, waiting for transfers between devices, shards(): lax.all_gather(tokens, 'tp', axis=1, tiled=True)  10 us
    all_gather x1, waiting for transfers between devices, shards(): lax.all_gather(cotangent, 'tp', axis=1, tiled=True)  5.55 us
    all_to_all x1, waiting for transfers between devices, shards(): lax.all_to_all(grad_rows, 'edp', split_axis=1, concat_axis=0, tiled=True)  5.29 us
    all_to_all x1, starting transfers between devices, shards(): lax.all_to_all(token_rows, 'edp', split_axis=1, concat_axis=0, tiled=True)  4.67 us
    all_to_all x1, waiting for transfers between devices, shards(): lax.all_to_all(scaled, 'ep', split_axis=0, concat_axis=0, tiled=True)  4.58 us
    all_to_all x1, starting transfers between devices, shards(): lax.all_to_all(grad_rows, 'edp', split_axis=1, concat_axis=0, tiled=True)  4.11 us
    all_to_all x1, starting transfers between devices, shards(): lax.all_to_all(packed, 'ep', split_axis=0, concat_axis=0, tiled=True)  3.92 us
  transfers between devices with their start and end apart: 10, of which 7 were waited for; matrix products, arithmetic and copies ran while one was open for 22% of the time, Pallas kernels for 0%

commit v1 on v0

--- a/solution.py
+++ b/solution.py
@@ -79,7 +79,12 @@
         lax.all_to_all(token_rows, "edp", split_axis=1, concat_axis=0, tiled=True),
         lax.all_to_all(grad_rows, "edp", split_axis=1, concat_axis=0, tiled=True),
     )
-    left_factors = lax.all_gather(jnp.stack([d_gate, d_up, hidden]), "edp", axis=1, tiled=True)
+    left_factors = jnp.concatenate(
+        lax.all_to_all(
+            jnp.stack([jnp.stack([d_gate, d_up, hidden])] * lax.axis_size("edp")), "edp", 0, 0
+        ),
+        axis=1,
+    )
     block_width = rows_block.shape[1]
     rows_block = rows_block.reshape(replicas, -1, block_width)
     grads_block = grads_block.reshape(replicas, -1, block_width)

time: 123 us -> 118 us (0.959)
  blocking collectives: 14.8 us -> 0 us
  waiting for transfers between devices: 33.9 us -> 40.3 us
  starting transfers between devices: 23.1 us -> 26.5 us
    all_gather x1 -> x0, blocking collectives: 14.8 us -> none  [shards(): lax.all_gather(jnp.stack([d_gate, d_up, hidden]), 'edp', axis=1, tiled=True)]
    all_to_all x0 -> x1, starting transfers between devices: none -> 4.67 us  [shards(): lax.all_to_all(jnp.stack([jnp.stack([d_gate, d_up, hidden])] * lax.axis_s...]
    all_to_all x1, waiting for transfers between devices: 0.01 us -> 3.56 us  [shards(): lax.all_to_all(token_rows, 'edp', split_axis=1, concat_axis=0, tiled=True)]
    all_to_all x0 -> x1, waiting for transfers between devices: none -> 3.19 us  [shards(): lax.all_to_all(jnp.stack([jnp.stack([d_gate, d_up, hidden])] * lax.axis_s...]
  transfers between devices with their start and end apart: 10 -> 11, of which waited for: 7 -> 9; matrix products, arithmetic and copies ran while one was open for 22% -> 25% of each run, Pallas kernels for 0% -> 0%
where the time goes in v1:
time: 118 us; the launch traced here: 117 us
  waiting for transfers between devices  40.3 us (34%)
  starting transfers between devices  26.5 us (22%)
  matrix products  22.5 us (19%)
  between operations  14 us (12%)
  local copies, waits for them, and re-layouts  8.8 us (7%)
  other arithmetic  5.3 us (4%)
    all_gather x1, waiting for transfers between devices, shards(): lax.all_gather(tokens, 'tp', axis=1, tiled=True)  10 us
    all_gather x1, waiting for transfers between devices, shards(): lax.all_gather(cotangent, 'tp', axis=1, tiled=True)  5.55 us
    all_to_all x1, waiting for transfers between devices, shards(): lax.all_to_all(grad_rows, 'edp', split_axis=1, concat_axis=0, tiled=True)  5.21 us
    all_to_all x1, starting transfers between devices, shards(): lax.all_to_all(jnp.stack([jnp.stack([d_gate, d_up, hidden])] * lax.axis_s...  4.67 us
    all_to_all x1, waiting for transfers between devices, shards(): lax.all_to_all(scaled, 'ep', split_axis=0, concat_axis=0, tiled=True)  4.6 us
    all_to_all x1, starting transfers between devices, shards(): lax.all_to_all(grad_rows, 'edp', split_axis=1, concat_axis=0, tiled=True)  4.09 us
    all_to_all x1, starting transfers between devices, shards(): lax.all_to_all(packed, 'ep', split_axis=0, concat_axis=0, tiled=True)  3.92 us
    dot_general x3, matrix products, replica_sum(): jnp.einsum('prs,prd->psd', left, right, preferred_element_type=jnp.float32)  3.76 us
  transfers between devices with their start and end apart: 11, of which 9 were waited for; matrix products, arithmetic and copies ran while one was open for 25% of the time, Pallas kernels for 0%

profile of v1, /device:TPU:0, one launch (start us, length us, event | category | flops | bytes accessed | tf_op | source)
XLA Modules:
  0.0 117.4 jit_solution(13325426099358148866)
XLA Ops:
  11.3 10.0 %all-gather.3.cloned.1.call-done = bf16[128,4096]{1,0:T(8,128)(2,1)} async-done(((bf16[128,2048]{1,0:T(8,128)(2,1)}), bf16[128,4096]{1,0:T(8,128)(2,1)}) %all-gather.3.cloned.1.call-update) | async-done | bytes 1048592 | tf_op jit(solution)/shard_map/all_gather | solution.py:43
  23.6 3.9 %all-to-all-start = ((bf16[4,10,4096]{2,1,0:T(8,128)(2,1)}), bf16[4,10,4096]{2,1,0:T(8,128)(2,1)S(1)}, u32[]{:S(2)}, u32[]{:S(2)}) async-start(bf16[4,10,4096]{2,1,0:T(8,128)(2,1)} %reshape.213), calls=%async_computation | async-start | bytes 1048576 | tf_op jit(solution)/shard_map/all_to_all | solution.py:48
  27.6 5.6 %all-gather.5.cloned.1.call-done = bf16[128,4096]{1,0:T(8,128)(2,1)} async-done(((bf16[128,2048]{1,0:T(8,128)(2,1)}), bf16[128,4096]{1,0:T(8,128)(2,1)}) %all-gather.5.cloned.1.call-update) | async-done | bytes 1048592 | tf_op jit(solution)/shard_map/all_gather | solution.py:44
  33.1 1.7 %convolution_convert_fusion.1 = bf16[10,4096]{1,0:T(8,128)(2,1)S(1)} fusion(f32[128,10]{0,1:T(8,128)S(1)} %get-tuple-element.4, bf16[128,4096]{1,0:T(8,128)(2,1)} %all-gather.5.cloned.1.call-done), kind=kOutput, calls=%fused_computation.3 | convolution fusion | flops 62955520 | bytes 1135616 | tf_op jit(solution)/shard_map/tec,td->ecd/dot_general | solution.py:26
  36.9 3.5 %all-to-all-start.2 = ((bf16[4,10,4096]{2,1,0:T(8,128)(2,1)}), bf16[4,10,4096]{2,1,0:T(8,128)(2,1)S(1)}, u32[]{:S(2)}, u32[]{:S(2)}) async-start(bf16[4,10,4096]{2,1,0:T(8,128)(2,1)} %reshape.216), calls=%async_computation.3 | async-start | bytes 1048576 | tf_op jit(solution)/shard_map/all_to_all | solution.py:49
  40.5 3.0 %fusion.13 = f32[2,40,192]{2,1,0:T(8,128)S(1)} fusion(bf16[40,4096,1]{1,0,2:T(8,128)(2,1)S(1)} %reshape.221, bf16[3,192,4096]{2,1,0:T(8,128)(2,1)} %param.9), kind=kOutput, calls=%fused_computation.26 | convolution fusion | flops 125829120 | bytes 3534848 | tf_op jit(solution)/shard_map/rd,jfd->jrf/dot_general | solution.py:54
  43.5 4.6 %all-to-all-done.2 = bf16[4,10,4096]{2,1,0:T(8,128)(2,1)S(1)} async-done(((bf16[4,10,4096]{2,1,0:T(8,128)(2,1)}), bf16[4,10,4096]{2,1,0:T(8,128)(2,1)S(1)}, u32[]{:S(2)}, u32[]{:S(2)}) %all-to-all-start.2) | async-done | bytes 327712 | tf_op jit(solution)/shard_map/all_to_all | solution.py:49
  48.2 2.0 %fusion.27 = (bf16[40,192]{1,0:T(8,128)(2,1)S(1)}, bf16[40,192]{1,0:T(8,128)(2,1)S(1)}) fusion(f32[2,40,192]{2,1,0:T(8,128)S(1)} %fusion.13, bf16[40,4096]{1,0:T(8,128)(2,1)S(1)} %reshape.217, bf16[3,192,4096]{2,1,0:T(8,128)(2,1)} %param.9), kind=kOutput, calls=%fused_computation.50 | convolution fusion | flops 63014400 | bytes 1992704 | tf_op jit(solution)/shard_map/dot_general | solution.py:67
  50.2 1.8 %fusion.4 = f32[40,4096]{1,0:T(8,128)S(1)} fusion(bf16[40,192]{1,0:T(8,128)(2,1)S(1)} %get-tuple-element.8, bf16[3,192,4096]{2,1,0:T(8,128)(2,1)} %param.9), kind=kOutput, calls=%fused_computation.17 | convolution fusion | flops 62914560 | bytes 2243584 | tf_op jit(solution)/shard_map/dot_general | solution.py:74
  52.8 4.7 %all-to-all-start.4 = ((bf16[4,3,40,192]{3,2,1,0:T(8,128)(2,1)}), bf16[4,3,40,192]{3,2,1,0:T(8,128)(2,1)S(1)}, u32[]{:S(2)}, u32[]{:S(2)}) async-start(bf16[4,3,40,192]{3,2,1,0:T(8,128)(2,1)} %stack.32), calls=%async_computation.6 | async-start | bytes 491520 | tf_op jit(solution)/shard_map/all_to_all | solution.py:83
  57.4 2.5 %fusion = bf16[40,4096]{1,0:T(8,128)(2,1)} fusion(f32[40,4096]{1,0:T(8,128)S(1)} %fusion.4, bf16[40,192]{1,0:T(8,128)(2,1)S(1)} %get-tuple-element.7, bf16[3,192,4096]{2,1,0:T(8,128)(2,1)} %param.9), kind=kOutput, calls=%fused_computation.1 | convolution fusion | flops 63242240 | bytes 2571264 | tf_op jit(solution)/shard_map/dot_general | solution.py:74
  61.0 3.2 %all-to-all-done.4 = bf16[4,3,40,192]{3,2,1,0:T(8,128)(2,1)S(1)} async-done(((bf16[4,3,40,192]{3,2,1,0:T(8,128)(2,1)}), bf16[4,3,40,192]{3,2,1,0:T(8,128)(2,1)S(1)}, u32[]{:S(2)}, u32[]{:S(2)}) %all-to-all-start.4) | async-done | bytes 184352 | tf_op jit(solution)/shard_map/all_to_all | solution.py:83
  64.2 3.5 %all-to-all-start.5 = ((bf16[40,4,1024]{2,0,1:T(8,128)(2,1)}), bf16[40,4,1024]{2,0,1:T(8,128)(2,1)S(1)}, u32[]{:S(2)}, u32[]{:S(2)}) async-start(bf16[40,4,1024]{2,0,1:T(8,128)(2,1)} %copy.41), calls=%async_computation.7 | async-start | bytes 655360 | tf_op jit(solution)/shard_map/all_to_all | solution.py:79
  68.8 2.5 %convolution_convert_fusion = bf16[40,4096]{1,0:T(8,128)(2,1)} fusion(bf16[3,192,4096]{2,1,0:T(8,128)(2,1)} %param.9, bf16[1,40,192]{2,1,0:T(8,128)(2,1)S(1)} %multiply_convert_fusion), kind=kOutput, calls=%fused_computation.2 | convolution fusion | flops 63078400 | bytes 1915904 | tf_op jit(solution)/shard_map/dot_general | solution.py:65
  71.4 3.6 %all-to-all-done.5 = bf16[40,4,1024]{2,0,1:T(8,128)(2,1)S(1)} async-done(((bf16[40,4,1024]{2,0,1:T(8,128)(2,1)}), bf16[40,4,1024]{2,0,1:T(8,128)(2,1)S(1)}, u32[]{:S(2)}, u32[]{:S(2)}) %all-to-all-start.5) | async-done | bytes 327712 | tf_op jit(solution)/shard_map/all_to_all | solution.py:79
  74.9 4.1 %all-to-all-start.6 = ((bf16[40,4,1024]{2,0,1:T(8,128)(2,1)}), bf16[40,4,1024]{2,0,1:T(8,128)(2,1)}, u32[]{:S(2)}, u32[]{:S(2)}) async-start(bf16[40,4,1024]{2,0,1:T(8,128)(2,1)} %copy.42), calls=%async_computation.8 | async-start | bytes 655360 | tf_op jit(solution)/shard_map/all_to_all | solution.py:80
  81.2 5.2 %all-to-all-done.6 = bf16[40,4,1024]{2,0,1:T(8,128)(2,1)} async-done(((bf16[40,4,1024]{2,0,1:T(8,128)(2,1)}), bf16[40,4,1024]{2,0,1:T(8,128)(2,1)}, u32[]{:S(2)}, u32[]{:S(2)}) %all-to-all-start.6) | async-done | bytes 327712 | tf_op jit(solution)/shard_map/all_to_all | solution.py:80
  91.5 3.4 %all-to-all-start.3 = ((bf16[4,10,2048]{2,1,0:T(8,128)(2,1)}), bf16[4,10,2048]{2,1,0:T(8,128)(2,1)S(1)}, u32[]{:S(2)}, u32[]{:S(2)}) async-start(bf16[4,10,2048]{2,1,0:T(8,128)(2,1)} %reshape.218), calls=%async_computation.5 | async-start | bytes 524288 | tf_op jit(solution)/shard_map/all_to_all | solution.py:115
  96.5 1.7 %reshape.215 = bf16[4,10,2048]{2,1,0:T(8,128)(2,1)} reshape(bf16[40,2048]{1,0:T(8,128)(2,1)} %reduce-scatter.3.cloned.1.call-done) | data formatting | bytes 327680 | tf_op jit(solution)/shard_map/reshape | solution.py:109
  98.1 2.1 %all-to-all-done.3 = bf16[4,10,2048]{2,1,0:T(8,128)(2,1)S(1)} async-done(((bf16[4,10,2048]{2,1,0:T(8,128)(2,1)}), bf16[4,10,2048]{2,1,0:T(8,128)(2,1)S(1)}, u32[]{:S(2)}, u32[]{:S(2)}) %all-to-all-start.3) | async-done | bytes 163872 | tf_op jit(solution)/shard_map/all_to_all | solution.py:115
  100.3 3.4 %all-to-all-start.1 = ((bf16[4,10,2048]{2,1,0:T(8,128)(2,1)}), bf16[4,10,2048]{2,1,0:T(8,128)(2,1)S(1)}, u32[]{:S(2)}, u32[]{:S(2)}) async-start(bf16[4,10,2048]{2,1,0:T(8,128)(2,1)} %reshape.215), calls=%async_computation.2 | async-start | bytes 524288 | tf_op jit(solution)/shard_map/all_to_all | solution.py:108
  103.7 1.8 %convolution_convert_fusion.3 = bf16[128,2048]{1,0:T(8,128)(2,1)} fusion(f32[128,10]{0,1:T(8,128)S(1)} %get-tuple-element.3, f32[10,2048]{1,0:T(8,128)S(1)} %convert_reduce_fusion.3), kind=kOutput, calls=%fused_computation.10 | convolution fusion | flops 31719424 | bytes 611328 | tf_op jit(solution)/shard_map/tec,ecd->td/dot_general | solution.py:128
  105.6 3.5 %all-to-all-done.1 = bf16[4,10,2048]{2,1,0:T(8,128)(2,1)S(1)} async-done(((bf16[4,10,2048]{2,1,0:T(8,128)(2,1)}), bf16[4,10,2048]{2,1,0:T(8,128)(2,1)S(1)}, u32[]{:S(2)}, u32[]{:S(2)}) %all-to-all-start.1) | async-done | bytes 163872 | tf_op jit(solution)/shard_map/all_to_all | solution.py:108
  109.1 1.8 %convolution_convert_fusion.4 = bf16[128,2048]{1,0:T(8,128)(2,1)} fusion(f32[128,10]{0,1:T(8,128)S(1)} %get-tuple-element.4, f32[10,2048]{1,0:T(8,128)S(1)} %convert_reduce_fusion.4), kind=kOutput, calls=%fused_computation.11 | convolution fusion | flops 31719424 | bytes 611328 | tf_op jit(solution)/shard_map/tec,ecd->td/dot_general | solution.py:125
  (53 shorter events, 20.4 us)
Async XLA Ops:
  7.2 14.2 %all-gather.3.cloned.1.call-start = ((), (), s32[]{:S(2)}) async-start(), calls=%async_computation.9 | async-start | bytes 1572864 | tf_op jit(solution)/shard_map/all_gather | solution.py:43
  7.9 25.2 %all-gather.5.cloned.1.call-start = ((), (), s32[]{:S(2)}) async-start(), calls=%async_computation.11 | async-start | bytes 1572864 | tf_op jit(solution)/shard_map/all_gather | solution.py:44
  23.6 12.4 %all-to-all-start = ((bf16[4,10,4096]{2,1,0:T(8,128)(2,1)}), bf16[4,10,4096]{2,1,0:T(8,128)(2,1)S(1)}, u32[]{:S(2)}, u32[]{:S(2)}) async-start(bf16[4,10,4096]{2,1,0:T(8,128)(2,1)} %reshape.213), calls=%async_computation | async-start | bytes 1048576 | tf_op jit(solution)/shard_map/all_to_all | solution.py:48
  36.9 11.2 %all-to-all-start.2 = ((bf16[4,10,4096]{2,1,0:T(8,128)(2,1)}), bf16[4,10,4096]{2,1,0:T(8,128)(2,1)S(1)}, u32[]{:S(2)}, u32[]{:S(2)}) async-start(bf16[4,10,4096]{2,1,0:T(8,128)(2,1)} %reshape.216), calls=%async_computation.3 | async-start | bytes 1048576 | tf_op jit(solution)/shard_map/all_to_all | solution.py:49
  52.8 11.5 %all-to-all-start.4 = ((bf16[4,3,40,192]{3,2,1,0:T(8,128)(2,1)}), bf16[4,3,40,192]{3,2,1,0:T(8,128)(2,1)S(1)}, u32[]{:S(2)}, u32[]{:S(2)}) async-start(bf16[4,3,40,192]{3,2,1,0:T(8,128)(2,1)} %stack.32), calls=%async_computation.6 | async-start | bytes 491520 | tf_op jit(solution)/shard_map/all_to_all | solution.py:83
  57.4 32.4 %reduce-scatter.5.cloned.1.call-start = ((), (), s32[]{:S(2)}) async-start(), calls=%async_computation.12 | async-start | bytes 491520 | tf_op jit(solution)/shard_map/reduce_scatter | solution.py:103
  64.2 10.7 %all-to-all-start.5 = ((bf16[40,4,1024]{2,0,1:T(8,128)(2,1)}), bf16[40,4,1024]{2,0,1:T(8,128)(2,1)S(1)}, u32[]{:S(2)}, u32[]{:S(2)}) async-start(bf16[40,4,1024]{2,0,1:T(8,128)(2,1)} %copy.41), calls=%async_computation.7 | async-start | bytes 655360 | tf_op jit(solution)/shard_map/all_to_all | solution.py:79
  67.7 28.8 %reduce-scatter.3.cloned.1.call-start = ((), (), s32[]{:S(2)}) async-start(), calls=%async_computation.10 | async-start | bytes 491520 | tf_op jit(solution)/shard_map/reduce_scatter | solution.py:100
  71.4 7.7 %copy-start.1 = (bf16[4,3,40,192]{3,2,0,1:T(8,128)(2,1)}, bf16[4,3,40,192]{3,2,0,1:T(8,128)(2,1)S(1)}, u32[]{:S(2)}) copy-start(bf16[4,3,40,192]{3,2,0,1:T(8,128)(2,1)S(1)} %copy.44) | copy-start | bytes 552964
  74.9 11.5 %all-to-all-start.6 = ((bf16[40,4,1024]{2,0,1:T(8,128)(2,1)}), bf16[40,4,1024]{2,0,1:T(8,128)(2,1)}, u32[]{:S(2)}, u32[]{:S(2)}) async-start(bf16[40,4,1024]{2,0,1:T(8,128)(2,1)} %copy.42), calls=%async_computation.8 | async-start | bytes 655360 | tf_op jit(solution)/shard_map/all_to_all | solution.py:80
  89.2 5.7 %copy-start = (f32[192,1024]{1,0:T(8,128)S(1)}, f32[192,1024]{1,0:T(8,128)}, u32[]{:S(2)}) copy-start(f32[192,1024]{1,0:T(8,128)} %convert_reduce_fusion.2) | copy-start | bytes 2359300
  91.5 8.8 %all-to-all-start.3 = ((bf16[4,10,2048]{2,1,0:T(8,128)(2,1)}), bf16[4,10,2048]{2,1,0:T(8,128)(2,1)S(1)}, u32[]{:S(2)}, u32[]{:S(2)}) async-start(bf16[4,10,2048]{2,1,0:T(8,128)(2,1)} %reshape.218), calls=%async_computation.5 | async-start | bytes 524288 | tf_op jit(solution)/shard_map/all_to_all | solution.py:115
  100.3 8.8 %all-to-all-start.1 = ((bf16[4,10,2048]{2,1,0:T(8,128)(2,1)}), bf16[4,10,2048]{2,1,0:T(8,128)(2,1)S(1)}, u32[]{:S(2)}, u32[]{:S(2)}) async-start(bf16[4,10,2048]{2,1,0:T(8,128)(2,1)} %reshape.215), calls=%async_computation.2 | async-start | bytes 524288 | tf_op jit(solution)/shard_map/all_to_all | solution.py:108
Sparse Core Ops, SparseCore 0:
  9.5 11.7 all-gather.2
  22.9 10.1 all-gather.4
  61.0 8.2 reduce-scatter.4
  72.0 8.8 reduce-scatter.2
